TPU v7x, 32 devices: a whole 2x2x4 slice. The times are simulated.
32 devices in a mesh: groups: 2 (over y), plane: 4 (over z), depth: 2 (over x), tok: 2 (over core).
Axes of the slice: x: 2, y: 2, z: 4, core: 2. Of those that a mesh axis runs over, the one named last changes fastest.
Arguments:
- tokens: bfloat16 [256, 2048], P(('groups', 'plane', 'depth', 'tok')), parts along dimension 0, may hold values from -6 to 6
- expert_ids: int32 [256, 4], P(('groups', 'plane', 'depth', 'tok')), parts along dimension 0, may hold values from 0 to 3, as said below
- slot_index: int32 [256, 4], P(('groups', 'plane', 'depth', 'tok')), parts along dimension 0, may hold values from 0 to 7, as said below
- route_weight: bfloat16 [256, 4], P(('groups', 'plane', 'depth', 'tok')), parts along dimension 0, may hold values from 0.099609375 to 1
- shared_gate: bfloat16 [2048], replicated, may hold values from -0.125 to 0.125
- shared_gate_up: bfloat16 [2, 2048, 5632], P(None, None, 'plane'), may hold values from -0.125 to 0.125
- shared_down: bfloat16 [5632, 2048], P('plane'), may hold values from -0.078125 to 0.078125
- expert_gate_up: bfloat16 [4, 2, 2048, 1408], P('plane', None, None, ('depth', 'tok')), may hold values from -0.125 to 0.125
- expert_down: bfloat16 [4, 1408, 2048], P('plane', ('depth', 'tok')), may hold values from -0.15625 to 0.15625
Outputs:
- mixed: bfloat16 [256, 2048], P(('groups', 'plane', 'depth', 'tok')), parts along dimension 0
There are 2 independent parts, one for each index of `groups`. A program takes and returns all parts, laid end to end along the dimension named above; an argument that names none is the same for every part. Nothing has to cross between parts.
Inputs may be any that keep to these rules, and one draw needn't show every extreme that they name: `expert_ids`: each row names 4 different experts. Among the choices of the rows of one device that name the same expert, slot_index takes each value from 0 to their count minus one exactly once, in an order that varies from draw to draw; the capacity 8 is filled on some devices.
All inputs are finite; a program needn't handle non-finite values.
Results may differ from a plain program's by a relative error of at most 0.019.
Values may be sent and summed in bfloat16 or wider, within the bound.
A program may use at most 64 MiB of HBM per device.

v0:
```python
import jax
import jax.numpy as jnp
from jax import lax
from jax.sharding import PartitionSpec as P


def gated_rows(token_rows, gate_up):
    gate_part = jnp.dot(token_rows, gate_up[0], preferred_element_type=jnp.float32)
    up_part = jnp.dot(token_rows, gate_up[1], preferred_element_type=jnp.float32)
    return (jax.nn.silu(gate_part) * up_part).astype(jnp.bfloat16)


def expert_rows(received, gate_up, down_proj):
    hidden = gated_rows(lax.all_gather(received, ("depth", "tok"), axis=0, tiled=True), gate_up)
    return lax.psum_scatter(
        jnp.dot(hidden, down_proj, preferred_element_type=jnp.float32).astype(jnp.bfloat16),
        ("depth", "tok"),
        scatter_dimension=0,
        tiled=True,
    ).astype(jnp.float32)


def on_device(
    tokens,
    expert_ids,
    slot_index,
    route_weight,
    shared_gate,
    shared_gate_up,
    shared_down,
    expert_gate_up,
    expert_down,
):
    planes = lax.axis_size("plane")
    tok_rows = tokens.shape[0]
    choose_count = expert_ids.shape[1]
    model_width = tokens.shape[1]
    capacity = max(2, tok_rows * choose_count // planes)
    slot_total = planes * capacity
    local_gate_up = expert_gate_up[0]
    local_down = expert_down[0]
    column = lax.broadcasted_iota(jnp.int32, (slot_total, 1, 1), 0)
    kept_mask = slot_index < capacity
    target = jnp.where(kept_mask, expert_ids * capacity + slot_index, -1)
    matches = target[None, :, :] == column
    spread = jnp.any(matches, axis=2).astype(jnp.bfloat16)
    outgoing = jnp.dot(spread, tokens, preferred_element_type=jnp.float32).astype(jnp.bfloat16)
    outgoing = outgoing.reshape(planes, capacity, model_width)
    routed_slots = lax.all_to_all(
        expert_rows(
            lax.all_to_all(outgoing, "plane", split_axis=0, concat_axis=0, tiled=True),
            local_gate_up,
            local_down,
        ).astype(jnp.bfloat16),
        "plane",
        split_axis=0,
        concat_axis=0,
        tiled=True,
    ).astype(jnp.float32)
    weights = route_weight.astype(jnp.float32)
    combine = jnp.sum(jnp.where(matches, weights[None, :, :], 0.0), axis=2).T
    routed = jnp.dot(
        combine,
        routed_slots.reshape(slot_total, model_width),
        precision=lax.Precision.HIGHEST,
        preferred_element_type=jnp.float32,
    )
    shared_hidden = gated_rows(lax.all_gather(tokens, "plane", axis=0, tiled=True), shared_gate_up)
    shared_out = lax.psum_scatter(
        jnp.dot(shared_hidden, shared_down, preferred_element_type=jnp.float32).astype(
            jnp.bfloat16
        ),
        "plane",
        scatter_dimension=0,
        tiled=True,
    ).astype(jnp.float32)
    shared_scale = jax.nn.sigmoid(jnp.dot(tokens, shared_gate, preferred_element_type=jnp.float32))
    result = shared_scale[:, None] * shared_out + routed
    return result.astype(jnp.bfloat16)


def solution(mesh):
    in_specs = (
        P(("groups", "plane", "depth", "tok"), None),
        P(("groups", "plane", "depth", "tok"), None),
        P(("groups", "plane", "depth", "tok"), None),
        P(("groups", "plane", "depth", "tok"), None),
        P(),
        P(None, None, "plane"),
        P("plane", None),
        P("plane", None, None, ("depth", "tok")),
        P("plane", ("depth", "tok"), None),
    )
    out_specs = P(("groups", "plane", "depth", "tok"), None)
    return jax.shard_map(
        on_device, mesh=mesh, in_specs=in_specs, out_specs=out_specs, check_vma=False
    )
```

profile of v0, /device:TPU:0, one launch (start us, length us, event | category | flops | bytes accessed | tf_op | source)
XLA Modules:
  0.0 94.5 jit_solution(18416283824460108339)
XLA Ops:
  6.5 0.0 copy-start
  6.5 0.8 add_select_fusion
  7.4 0.1 fusion.48
  7.4 1.6 %fusion.12 = bf16[4,8,2048]{2,1,0:T(8,128)(2,1)} fusion(pred[32,8]{0,1:T(8,128)(4,1)S(1)} %fusion.48, bf16[8,2048]{1,0:T(8,128)(2,1)} %param.9), kind=kOutput, calls=%fused_computation.11 | convolution fusion | flops 1114112 | bytes 164096 | tf_op jit(solution)/shard_map/dot_general | solution.py:47
  9.1 6.3 %all-to-all-start = ((bf16[4,8,2048]{2,1,0:T(8,128)(2,1)}), bf16[4,8,2048]{2,1,0:T(8,128)(2,1)S(1)}, u32[]{:S(2)}, u32[]{:S(2)}) async-start(bf16[4,8,2048]{2,1,0:T(8,128)(2,1)} %fusion.12), calls=%async_computation.1 | async-start | bytes 262144 | tf_op jit(solution)/shard_map/all_to_all | solution.py:51
  15.4 0.0 reduce-scatter.5.cloned.1.call-start
  15.4 14.1 %all_gather.6 = bf16[32,2048]{1,0:T(8,128)(2,1)S(1)} all-gather(bf16[8,2048]{1,0:T(8,128)(2,1)} %param.9), channel_id=1, replica_groups=mesh['groups'=2,'plane'=4,'depth'=2,'tok'=2] {'plane'}, dimensions={0}, use_global_device_ids=true | all-gather | bytes 163840 | tf_op jit(solution)/shard_map/all_gather | solution.py:68
  29.6 0.0 all-to-all-done
  29.6 7.2 %all_gather.7 = bf16[16,8,2048]{2,1,0:T(8,128)(2,1)S(1)} all-gather(bf16[4,8,2048]{2,1,0:T(8,128)(2,1)S(1)} %all-to-all-done), channel_id=1, replica_groups=mesh['groups'=2,'plane'=4,'depth'=2,'tok'=2] {'depth','tok'}, dimensions={0}, use_global_device_ids=true | all-gather | bytes 655360 | tf_op jit(solution)/shard_map/all_gather | solution.py:14
  36.7 2.0 %fusion.16 = f32[16,8,352]{2,1,0:T(8,128)S(1)} fusion(bf16[16,8,2048]{2,1,0:T(8,128)(2,1)S(1)} %all_gather.7, bf16[1,2,2048,352]{2,3,1,0:T(8,128)(2,1)} %param.16), kind=kOutput, calls=%fused_computation.16 | convolution fusion | flops 184549376 | bytes 2146304 | tf_op jit(solution)/shard_map/dot_general | solution.py:8
  38.7 0.0 copy-done
  38.7 3.4 %convolution_convert_fusion = bf16[16,8,2048]{2,1,0:T(8,128)(2,1)} fusion(bf16[1,352,2048]{2,1,0:T(8,128)(2,1)S(1)} %copy-done, bf16[16,8,2048]{2,1,0:T(8,128)(2,1)S(1)} %all_gather.7, bf16[1,2,2048,352]{2,3,1,0:T(8,128)(2,1)} %param.16, f32[16,8,352]{2,1,0:T(8,128)S(1)} %fusion.16), kind=kOutput, calls=%fused_computation.6 | convolution fusion | flops 369631232 | bytes 4112384 | tf_op jit(solution)/shard_map/dot_general | solution.py:16
  42.1 0.0 reduce-scatter.5.cloned.1.call-update
  42.1 0.0 reduce-scatter.3.cloned.1.call-start
  42.2 3.7 %fusion.2 = f32[32,1408]{1,0:T(8,128)S(1)} fusion(bf16[32,2048]{1,0:T(8,128)(2,1)S(1)} %all_gather.6, bf16[2,2048,1408]{2,1,0:T(8,128)(2,1)} %param.14), kind=kOutput, calls=%fused_computation.2 | convolution fusion | flops 184549376 | bytes 6078464 | tf_op jit(solution)/shard_map/dot_general | solution.py:8
  45.8 0.0 copy-start.3
  45.8 0.0 copy-start.2
  45.9 0.0 copy-start.1
  45.9 7.2 %convolution_convert_fusion.2 = bf16[32,2048]{1,0:T(8,128)(2,1)} fusion(bf16[1408,2048]{1,0:T(8,128)(2,1)} %param.15, bf16[32,2048]{1,0:T(8,128)(2,1)S(1)} %all_gather.6, bf16[2,2048,1408]{2,1,0:T(8,128)(2,1)} %param.14, f32[32,1408]{1,0:T(8,128)S(1)} %fusion.2), kind=kOutput, calls=%fused_computation.10 | convolution fusion | flops 369434624 | bytes 11976704 | tf_op jit(solution)/shard_map/dot_general | solution.py:70
  53.1 0.0 reduce-scatter.3.cloned.1.call-update
  53.1 0.0 copy-done.3
  53.1 0.1 select_reduce_fusion
  53.2 0.0 copy-done.2
  53.2 11.1 %reduce-scatter.5.cloned.1.call-done = bf16[4,8,2048]{2,1,0:T(8,128)(2,1)} async-done(((bf16[16,8,2048]{2,1,0:T(8,128)(2,1)}), bf16[4,8,2048]{2,1,0:T(8,128)(2,1)}) %reduce-scatter.5.cloned.1.call-update) | async-done | bytes 131088 | tf_op jit(solution)/shard_map/reduce_scatter | solution.py:15
  64.3 4.6 %all-to-all-start.1 = ((bf16[4,8,2048]{2,1,0:T(8,128)(2,1)}), bf16[4,8,2048]{2,1,0:T(8,128)(2,1)S(1)}, u32[]{:S(2)}, u32[]{:S(2)}) async-start(bf16[4,8,2048]{2,1,0:T(8,128)(2,1)} %reduce-scatter.5.cloned.1.call-done), calls=%async_computation.3 | async-start | bytes 262144 | tf_op jit(solution)/shard_map/all_to_all | solution.py:49
  68.9 0.0 copy-done.1
  69.0 0.1 fusion.32
  69.1 17.0 %reduce-scatter.3.cloned.1.call-done = bf16[8,2048]{1,0:T(8,128)(2,1)} async-done(((bf16[32,2048]{1,0:T(8,128)(2,1)}), bf16[8,2048]{1,0:T(8,128)(2,1)}) %reduce-scatter.3.cloned.1.call-update) | async-done | bytes 32784 | tf_op jit(solution)/shard_map/reduce_scatter | solution.py:69
  86.1 0.0 all-to-all-done.1
  86.1 1.5 %fusion.13 = bf16[8,2048]{1,0:T(8,128)(2,1)} fusion(f32[32,8]{0,1:T(8,128)S(1)} %select_reduce_fusion, bf16[4,8,2048]{2,1,0:T(8,128)(2,1)S(1)} %all-to-all-done.1, bf16[8,2048]{1,0:T(8,128)(2,1)} %reduce-scatter.3.cloned.1.call-done, f32[8]{0:T(128)S(1)} %fusion.32), kind=kOutput, calls=%fused_computation.13 | convolution fusion | flops 6356992 | bytes 197664 | tf_op jit(solution)/shard_map/dot_general | solution.py:62
  (2 shorter events, 0.0 us)
Async XLA Ops:
  6.5 32.2 %copy-start = (bf16[1,352,2048]{2,1,0:T(8,128)(2,1)S(1)}, bf16[1,352,2048]{2,1,0:T(8,128)(2,1)}, u32[]{:S(2)}) copy-start(bf16[1,352,2048]{2,1,0:T(8,128)(2,1)} %param.17) | copy-start | bytes 4325380
  9.1 20.5 %all-to-all-start = ((bf16[4,8,2048]{2,1,0:T(8,128)(2,1)}), bf16[4,8,2048]{2,1,0:T(8,128)(2,1)S(1)}, u32[]{:S(2)}, u32[]{:S(2)}) async-start(bf16[4,8,2048]{2,1,0:T(8,128)(2,1)} %fusion.12), calls=%async_computation.1 | async-start | bytes 262144 | tf_op jit(solution)/shard_map/all_to_all | solution.py:51
  15.4 48.9 %reduce-scatter.5.cloned.1.call-start = ((), (), s32[]{:S(2)}) async-start(), calls=%async_computation.5 | async-start | bytes 655360 | tf_op jit(solution)/shard_map/reduce_scatter | solution.py:15
  42.1 44.0 %reduce-scatter.3.cloned.1.call-start = ((), (), s32[]{:S(2)}) async-start(), calls=%async_computation.4 | async-start | bytes 163840 | tf_op jit(solution)/shard_map/reduce_scatter | solution.py:69
  45.8 7.3 %copy-start.3 = (bf16[8,4]{0,1:T(4,128)(2,1)S(1)}, bf16[8,4]{0,1:T(4,128)(2,1)}, u32[]{:S(2)}) copy-start(bf16[8,4]{0,1:T(4,128)(2,1)} %param.12) | copy-start | bytes 196
  45.8 7.4 %copy-start.2 = (bf16[2048]{0:T(1024)(128)(2,1)S(1)}, bf16[2048]{0:T(1024)(128)(2,1)}, u32[]{:S(2)}) copy-start(bf16[2048]{0:T(1024)(128)(2,1)} %param.13) | copy-start | bytes 12292
  45.9 23.1 %copy-start.1 = (bf16[8,2048]{1,0:T(8,128)(2,1)S(1)}, bf16[8,2048]{1,0:T(8,128)(2,1)}, u32[]{:S(2)}) copy-start(bf16[8,2048]{1,0:T(8,128)(2,1)} %param.9) | copy-start | bytes 98308
  64.3 21.7 %all-to-all-start.1 = ((bf16[4,8,2048]{2,1,0:T(8,128)(2,1)}), bf16[4,8,2048]{2,1,0:T(8,128)(2,1)S(1)}, u32[]{:S(2)}, u32[]{:S(2)}) async-start(bf16[4,8,2048]{2,1,0:T(8,128)(2,1)} %reduce-scatter.5.cloned.1.call-done), calls=%async_computation.3 | async-start | bytes 262144 | tf_op jit(solution)/shard_map/all_to_all | solution.py:49
Sparse Core Ops, SparseCore 0:
  42.2 22.0 reduce-scatter.4
  66.6 19.4 reduce-scatter.2
where the time goes:
time: 95 us; the launch traced here: 94.5 us
  waiting for transfers between devices  28.1 us (30%)
  blocking collectives  21.3 us (22%)
  matrix products  19.5 us (21%)
  between operations  13.5 us (14%)
  starting transfers between devices  11 us (12%)
  other arithmetic  0.97 us (1%)
    reduce_scatter x1, waiting for transfers between devices, on_device(): lax.psum_scatter(jnp.dot(shared_hidden, shared_down, preferred_element_ty...  17 us
    all_gather x1, blocking collectives, on_device(): lax.all_gather(tokens, 'plane', axis=0, tiled=True)  14.1 us
    reduce_scatter x1, waiting for transfers between devices, expert_rows(): lax.psum_scatter(jnp.dot(hidden, down_proj, preferred_element_type=jnp.fl...  11.1 us
    dot_general x1, matrix products, on_device(): jnp.dot(shared_hidden, shared_down, preferred_element_type=jnp.float32)  7.22 us
    all_gather x1, blocking collectives, expert_rows(): lax.all_gather(received, ('depth', 'tok'), axis=0, tiled=True)  7.16 us
    all_to_all x1, starting transfers between devices, on_device(): lax.all_to_all(outgoing, 'plane', split_axis=0, concat_axis=0, tiled=True)  6.35 us
    dot_general x2, matrix products, gated_rows(): jnp.dot(token_rows, gate_up[0], preferred_element_type=jnp.float32)  5.62 us
    all_to_all x1, starting transfers between devices, on_device(): lax.all_to_all(expert_rows(lax.all_to_all(outgoing, 'plane', split_axis=0...  4.6 us
  transfers between devices with their start and end apart: 4, of which 2 were waited for; matrix products, arithmetic and copies ran while one was open for 12% of the time, Pallas kernels for 0%

commit v1 on v0

--- a/solution.py
+++ b/solution.py
@@ -2,6 +2,18 @@
 import jax.numpy as jnp
 from jax import lax
 from jax.sharding import PartitionSpec as P
+
+
+def collect(x, axis, dim):
+    ways, here = (lax.axis_size(axis), lax.axis_index(axis))
+    grown, reach = (x, 1)
+    while reach < ways:
+        theirs = lax.ppermute(grown, axis, [(d, d ^ reach) for d in range(ways)])
+        mine_first = jnp.concatenate([grown, theirs], axis=dim)
+        theirs_first = jnp.concatenate([theirs, grown], axis=dim)
+        grown = jnp.where(here & reach == 0, mine_first, theirs_first)
+        reach = 2 * reach
+    return grown
 
 
 def gated_rows(token_rows, gate_up):
@@ -11,7 +23,7 @@
 
 
 def expert_rows(received, gate_up, down_proj):
-    hidden = gated_rows(lax.all_gather(received, ("depth", "tok"), axis=0, tiled=True), gate_up)
+    hidden = gated_rows(collect(received, ("depth", "tok"), 0), gate_up)
     return lax.psum_scatter(
         jnp.dot(hidden, down_proj, preferred_element_type=jnp.float32).astype(jnp.bfloat16),
         ("depth", "tok"),

time: 95 us -> 93.2 us (0.981)
  starting transfers between devices: 11 us -> 6.21 us
  blocking collectives: 21.3 us -> 25.9 us
    all_to_all x0 -> x1, blocking collectives: none -> 12.2 us  [on_device(): lax.all_to_all(outgoing, 'plane', split_axis=0, concat_axis=0, tiled=True)]
    all_gather x1 -> x0, blocking collectives: 7.16 us -> none  [expert_rows(): lax.all_gather(received, ('depth', 'tok'), axis=0, tiled=True)]
    all_to_all x1 -> x0, starting transfers between devices: 6.35 us -> none  [on_device(): lax.all_to_all(outgoing, 'plane', split_axis=0, concat_axis=0, tiled=True)]
    reduce_scatter x1, waiting for transfers between devices: 11.1 us -> 8.87 us  [expert_rows(): lax.psum_scatter(jnp.dot(hidden, down_proj, preferred_element_type=jnp.fl...]
    dot_general x0 -> x1, matrix products: none -> 1.97 us  [gated_rows(): jnp.dot(token_rows, gate_up[1], preferred_element_type=jnp.float32)]
    dot_general x2 -> x1, matrix products: 5.62 us -> 3.66 us  [gated_rows(): jnp.dot(token_rows, gate_up[0], preferred_element_type=jnp.float32)]
    ppermute x0 -> x2, starting transfers between devices: none -> 1.56 us  [collect(): theirs = lax.ppermute(grown, axis, [(d, d ^ reach) for d in range(ways)])]
    ppermute x0 -> x2, waiting for transfers between devices: none -> 1.35 us  [collect(): theirs = lax.ppermute(grown, axis, [(d, d ^ reach) for d in range(ways)])]
  transfers between devices with their start and end apart: 4 -> 5, of which waited for: 2 -> 3; matrix products, arithmetic and copies ran while one was open for 12% -> 12% of each run, Pallas kernels for 0% -> 0%
where the time goes in v1:
time: 93.2 us; the launch traced here: 92.8 us
  waiting for transfers between devices  27.2 us (29%)
  blocking collectives  25.9 us (28%)
  matrix products  18.9 us (20%)
  between operations  13.5 us (14%)
  starting transfers between devices  6.21 us (7%)
  other arithmetic  1 us (1%)
    reduce_scatter x1, waiting for transfers between devices, on_device(): lax.psum_scatter(jnp.dot(shared_hidden, shared_down, preferred_element_ty...  17 us
    all_gather x1, blocking collectives, on_device(): lax.all_gather(tokens, 'plane', axis=0, tiled=True)  13.7 us
    all_to_all x1, blocking collectives, on_device(): lax.all_to_all(outgoing, 'plane', split_axis=0, concat_axis=0, tiled=True)  12.2 us
    reduce_scatter x1, waiting for transfers between devices, expert_rows(): lax.psum_scatter(jnp.dot(hidden, down_proj, preferred_element_type=jnp.fl...  8.87 us
    dot_general x1, matrix products, on_device(): jnp.dot(shared_hidden, shared_down, preferred_element_type=jnp.float32)  7.23 us
    all_to_all x1, starting transfers between devices, on_device(): lax.all_to_all(expert_rows(lax.all_to_all(outgoing, 'plane', split_axis=0...  4.6 us
    dot_general x1, matrix products, gated_rows(): jnp.dot(token_rows, gate_up[0], preferred_element_type=jnp.float32)  3.66 us
    dot_general x1, matrix products, expert_rows(): jnp.dot(hidden, down_proj, preferred_element_type=jnp.float32)  3.4 us
  transfers between devices with their start and end apart: 5, of which 3 were waited for; matrix products, arithmetic and copies ran while one was open for 12% of the time, Pallas kernels for 0%

profile of v1, /device:TPU:0, one launch (start us, length us, event | category | flops | bytes accessed | tf_op | source)
XLA Modules:
  0.0 92.8 jit_solution(9442800633254162574)
XLA Ops:
  6.5 0.0 copy-start
  6.5 0.0 reduce-scatter.5.cloned.1.call-start
  6.5 0.8 add_select_fusion
  7.4 0.1 fusion.39
  7.4 1.0 %fusion.12 = bf16[4,8,2048]{2,1,0:T(8,128)(2,1)S(1)} fusion(pred[32,8]{0,1:T(8,128)(4,1)S(1)} %fusion.39, bf16[8,2048]{1,0:T(8,128)(2,1)} %param.9), kind=kOutput, calls=%fused_computation.11 | convolution fusion | flops 1114112 | bytes 164096 | tf_op jit(solution)/shard_map/dot_general | solution.py:59
  8.4 12.2 %all_to_all.10 = bf16[4,8,2048]{2,1,0:T(8,128)(2,1)S(1)} all-to-all(bf16[4,8,2048]{2,1,0:T(8,128)(2,1)S(1)} %fusion.12), channel_id=1, replica_groups=mesh['groups'=2,'plane'=4,'depth'=2,'tok'=2] {'plane'}, dimensions={0} | all-to-all | bytes 262144 | tf_op jit(solution)/shard_map/all_to_all | solution.py:63
  20.6 0.0 collective-permute-start
  20.6 1.3 %collective-permute-done = bf16[4,8,2048]{2,1,0:T(8,128)(2,1)S(1)} collective-permute-done((bf16[4,8,2048]{2,1,0:T(8,128)(2,1)S(1)}, bf16[4,8,2048]{2,1,0:T(8,128)(2,1)S(1)}, u32[]{:S(2)}, u32[]{:S(2)}) %collective-permute-start) | collective-permute-done | bytes 131104 | tf_op jit(solution)/shard_map/ppermute | solution.py:11
  22.0 1.6 %collective-permute-start.1 = (bf16[8,8,2048]{2,1,0:T(8,128)(2,1)S(1)}, bf16[8,8,2048]{2,1,0:T(8,128)(2,1)S(1)}, u32[]{:S(2)}, u32[]{:S(2)}) collective-permute-start(bf16[8,8,2048]{2,1,0:T(8,128)(2,1)S(1)} %maximum_select_fusion.1), channel_id=1, source_target_pairs={{0,2},{1,3},{2,0},{3,1},{4,6},{5,7},{6,4},{7,5},{8,10},{9,11},{10,... | collective-permute-start | bytes 786440 | tf_op jit(solution)/shard_map/ppermute | solution.py:11
  23.6 13.7 %all_gather.3 = bf16[32,2048]{1,0:T(8,128)(2,1)S(1)} all-gather(bf16[8,2048]{1,0:T(8,128)(2,1)} %param.9), channel_id=1, replica_groups=mesh['groups'=2,'plane'=4,'depth'=2,'tok'=2] {'plane'}, dimensions={0}, use_global_device_ids=true | all-gather | bytes 163840 | tf_op jit(solution)/shard_map/all_gather | solution.py:80
  37.2 0.0 collective-permute-done.1
  37.2 2.0 %fusion.14 = f32[16,8,352]{2,1,0:T(8,128)S(1)} fusion(bf16[1,2,2048,352]{2,3,1,0:T(8,128)(2,1)} %param.16, bf16[8,8,2048]{2,1,0:T(8,128)(2,1)S(1)} %collective-permute-done.1, bf16[8,8,2048]{2,1,0:T(8,128)(2,1)S(1)} %maximum_select_fusion.1, pred[]{:T(512)S(6)} %eq.22), kind=kOutput, calls=%fused_computation.14 | convolution fusion | flops 185335808 | bytes 2146305 | tf_op jit(solution)/shard_map/dot_general | solution.py:21
  39.2 0.0 copy-done
  39.2 3.4 %convolution_convert_fusion = bf16[16,8,2048]{2,1,0:T(8,128)(2,1)} fusion(bf16[1,352,2048]{2,1,0:T(8,128)(2,1)S(1)} %copy-done, f32[16,8,352]{2,1,0:T(8,128)S(1)} %fusion.14, bf16[1,2,2048,352]{2,3,1,0:T(8,128)(2,1)} %param.16, bf16[8,8,2048]{2,1,0:T(8,128)(2,1)S(1)} %collective-permute-done.1, bf16[8,8,2048]{2,1,0:T(8,128)(2,1)S(1)} %maximum_select_fusion.1, ...), kind=kOutput, calls=%fused_computation.6 | convolution fusion | flops 370417664 | bytes 4112385 | tf_op jit(solution)/shard_map/dot_general | solution.py:28
  42.6 0.0 reduce-scatter.5.cloned.1.call-update
  42.6 0.0 reduce-scatter.3.cloned.1.call-start
  42.7 3.7 %fusion.2 = f32[32,1408]{1,0:T(8,128)S(1)} fusion(bf16[32,2048]{1,0:T(8,128)(2,1)S(1)} %all_gather.3, bf16[2,2048,1408]{2,1,0:T(8,128)(2,1)} %param.14), kind=kOutput, calls=%fused_computation.2 | convolution fusion | flops 184549376 | bytes 6078464 | tf_op jit(solution)/shard_map/dot_general | solution.py:20
  46.4 0.0 copy-start.3
  46.4 0.0 copy-start.2
  46.4 0.0 copy-start.1
  46.4 7.2 %convolution_convert_fusion.2 = bf16[32,2048]{1,0:T(8,128)(2,1)} fusion(bf16[1408,2048]{1,0:T(8,128)(2,1)} %param.15, bf16[32,2048]{1,0:T(8,128)(2,1)S(1)} %all_gather.3, bf16[2,2048,1408]{2,1,0:T(8,128)(2,1)} %param.14, f32[32,1408]{1,0:T(8,128)S(1)} %fusion.2), kind=kOutput, calls=%fused_computation.10 | convolution fusion | flops 369434624 | bytes 11976704 | tf_op jit(solution)/shard_map/dot_general | solution.py:82
  53.6 0.0 reduce-scatter.3.cloned.1.call-update
  53.6 0.0 copy-done.3
  53.7 0.1 select_reduce_fusion
  53.7 0.0 copy-done.2
  53.8 8.9 %reduce-scatter.5.cloned.1.call-done = bf16[4,8,2048]{2,1,0:T(8,128)(2,1)} async-done(((bf16[16,8,2048]{2,1,0:T(8,128)(2,1)}), bf16[4,8,2048]{2,1,0:T(8,128)(2,1)}) %reduce-scatter.5.cloned.1.call-update) | async-done | bytes 131088 | tf_op jit(solution)/shard_map/reduce_scatter | solution.py:27
  62.6 4.6 %all-to-all-start.1 = ((bf16[4,8,2048]{2,1,0:T(8,128)(2,1)}), bf16[4,8,2048]{2,1,0:T(8,128)(2,1)S(1)}, u32[]{:S(2)}, u32[]{:S(2)}) async-start(bf16[4,8,2048]{2,1,0:T(8,128)(2,1)} %reduce-scatter.5.cloned.1.call-done), calls=%async_computation.3 | async-start | bytes 262144 | tf_op jit(solution)/shard_map/all_to_all | solution.py:61
  67.2 0.0 copy-done.1
  67.2 0.1 fusion.24
  67.4 17.0 %reduce-scatter.3.cloned.1.call-done = bf16[8,2048]{1,0:T(8,128)(2,1)} async-done(((bf16[32,2048]{1,0:T(8,128)(2,1)}), bf16[8,2048]{1,0:T(8,128)(2,1)}) %reduce-scatter.3.cloned.1.call-update) | async-done | bytes 32784 | tf_op jit(solution)/shard_map/reduce_scatter | solution.py:81
  84.4 0.0 all-to-all-done.1
  84.4 1.5 %fusion.13 = bf16[8,2048]{1,0:T(8,128)(2,1)} fusion(f32[32,8]{0,1:T(8,128)S(1)} %select_reduce_fusion, bf16[4,8,2048]{2,1,0:T(8,128)(2,1)S(1)} %all-to-all-done.1, bf16[8,2048]{1,0:T(8,128)(2,1)} %reduce-scatter.3.cloned.1.call-done, f32[8]{0:T(128)S(1)} %fusion.24), kind=kOutput, calls=%fused_computation.13 | convolution fusion | flops 6356992 | bytes 197664 | tf_op jit(solution)/shard_map/dot_general | solution.py:74
  (3 shorter events, 0.0 us)
Async XLA Ops:
  6.5 32.7 %copy-start = (bf16[1,352,2048]{2,1,0:T(8,128)(2,1)S(1)}, bf16[1,352,2048]{2,1,0:T(8,128)(2,1)}, u32[]{:S(2)}) copy-start(bf16[1,352,2048]{2,1,0:T(8,128)(2,1)} %param.17) | copy-start | bytes 4325380
  6.5 56.1 %reduce-scatter.5.cloned.1.call-start = ((), (), s32[]{:S(2)}) async-start(), calls=%async_computation.5 | async-start | bytes 655360 | tf_op jit(solution)/shard_map/reduce_scatter | solution.py:27
  20.6 1.3 %collective-permute-start = (bf16[4,8,2048]{2,1,0:T(8,128)(2,1)S(1)}, bf16[4,8,2048]{2,1,0:T(8,128)(2,1)S(1)}, u32[]{:S(2)}, u32[]{:S(2)}) collective-permute-start(bf16[4,8,2048]{2,1,0:T(8,128)(2,1)S(1)} %all_to_all.10), channel_id=1, source_target_pairs={{0,1},{1,0},{2,3},{3,2},{4,5},{5,4},{6,7},{7,6},{8,9},{9,8},{10,11... | collective-permute-start | bytes 393224 | tf_op jit(solution)/shard_map/ppermute | solution.py:11
  22.0 15.2 %collective-permute-start.1 = (bf16[8,8,2048]{2,1,0:T(8,128)(2,1)S(1)}, bf16[8,8,2048]{2,1,0:T(8,128)(2,1)S(1)}, u32[]{:S(2)}, u32[]{:S(2)}) collective-permute-start(bf16[8,8,2048]{2,1,0:T(8,128)(2,1)S(1)} %maximum_select_fusion.1), channel_id=1, source_target_pairs={{0,2},{1,3},{2,0},{3,1},{4,6},{5,7},{6,4},{7,5},{8,10},{9,11},{10,... | collective-permute-start | bytes 786440 | tf_op jit(solution)/shard_map/ppermute | solution.py:11
  42.6 41.7 %reduce-scatter.3.cloned.1.call-start = ((), (), s32[]{:S(2)}) async-start(), calls=%async_computation.4 | async-start | bytes 163840 | tf_op jit(solution)/shard_map/reduce_scatter | solution.py:81
  46.4 7.3 %copy-start.3 = (bf16[8,4]{0,1:T(4,128)(2,1)S(1)}, bf16[8,4]{0,1:T(4,128)(2,1)}, u32[]{:S(2)}) copy-start(bf16[8,4]{0,1:T(4,128)(2,1)} %param.12) | copy-start | bytes 196
  46.4 7.4 %copy-start.2 = (bf16[2048]{0:T(1024)(128)(2,1)S(1)}, bf16[2048]{0:T(1024)(128)(2,1)}, u32[]{:S(2)}) copy-start(bf16[2048]{0:T(1024)(128)(2,1)} %param.13) | copy-start | bytes 12292
  46.4 20.9 %copy-start.1 = (bf16[8,2048]{1,0:T(8,128)(2,1)S(1)}, bf16[8,2048]{1,0:T(8,128)(2,1)}, u32[]{:S(2)}) copy-start(bf16[8,2048]{1,0:T(8,128)(2,1)} %param.9) | copy-start | bytes 98308
  62.6 21.7 %all-to-all-start.1 = ((bf16[4,8,2048]{2,1,0:T(8,128)(2,1)}), bf16[4,8,2048]{2,1,0:T(8,128)(2,1)S(1)}, u32[]{:S(2)}, u32[]{:S(2)}) async-start(bf16[4,8,2048]{2,1,0:T(8,128)(2,1)} %reduce-scatter.5.cloned.1.call-done), calls=%async_computation.3 | async-start | bytes 262144 | tf_op jit(solution)/shard_map/all_to_all | solution.py:61
Sparse Core Ops, SparseCore 0:
  42.8 19.8 reduce-scatter.4
  64.9 19.4 reduce-scatter.2
